TPU v7x, 32 devices: a whole 2x2x4 slice. The times are simulated.
32 devices in a mesh: row: 8 (over z, core), col: 4 (over y, x).
Axes of the slice: x: 2, y: 2, z: 4, core: 2. Of those that a mesh axis runs over, the one named last changes fastest.
Arguments:
- right_side: float32 [1, 8, 4, 1024], P(None, 'row'), may hold values from -6 to 6
- inverse_t: bfloat16 [1, 8, 1024, 1024], P(None, 'row', 'col'), as said below
- u_factor: bfloat16 [1, 8, 2, 4, 128, 1024], P(None, 'row', None, 'col'), may hold values from -0.25 to 0.25
- v_factor: bfloat16 [1, 8, 2, 4, 128, 1024], P(None, 'row', None, 'col'), may hold values from -0.1875 to 0.1875
- ranks: int32 [1, 8, 2, 4], P(None, 'row', None, 'col'), may hold values from 4 to 128, as said below
Outputs:
- whitened: float32 [1, 8, 4, 1024], P(None, 'row')
- loglik: float32 [1, 8, 4], P(None, 'row')
Inputs may be any that keep to these rules, and one draw needn't show every extreme that they name: Tile (i, j) with j < i uses the first ranks of its factor rows. `inverse_t`: upper triangular with a positive diagonal.
All inputs are finite; a program needn't handle non-finite values.
Results may differ from a plain program's by a relative error of at most 0.0085.
Values sent between devices are 32-bit elements; how exact they have to be, the bound alone decides.
A program may use at most 64 MiB of HBM per device.

v0:
```python
import math

import jax
import jax.numpy as jnp
from jax import lax
from jax.sharding import PartitionSpec as P


def rank_part(v_tiles, u_tiles, rounded, limit):
    width = v_tiles.shape[1]
    inner = jnp.einsum("brn,bkn->brk", v_tiles, rounded, preferred_element_type=jnp.float32)
    keep = jnp.arange(width, dtype=jnp.int32)[None, :] < limit[:, None]
    inner = jnp.where(keep[:, :, None], inner, 0.0).astype(jnp.bfloat16)
    return jnp.einsum("brk,brn->bkn", inner, u_tiles, preferred_element_type=jnp.float32)


def project(v_tiles, u_tiles, rounded, limit):
    return rank_part(v_tiles, u_tiles, rounded, limit)


def local(right_side, inverse_t, u_factor, v_factor, ranks):
    n_row = lax.axis_size("row")
    n_col = lax.axis_size("col")
    cycles = right_side.shape[0]
    nrhs = right_side.shape[2]
    width = right_side.shape[3]
    slab = cycles * n_row
    per_col = slab // n_col
    piece = width // n_col
    rank_max = u_factor.shape[4]
    my_row = lax.axis_index("row")
    my_col = lax.axis_index("col")
    sources = right_side.reshape(cycles, nrhs, width)
    inverse = inverse_t.reshape(cycles, piece, width)
    u_tiles = u_factor.reshape(cycles, per_col, rank_max, width)
    v_tiles = v_factor.reshape(cycles, per_col, rank_max, width)
    limits = ranks.reshape(cycles, per_col)
    column_ids = jnp.arange(per_col, dtype=jnp.int32) * n_col + my_col
    block_start = my_col * piece

    def finish(partial_value, cycle, index):
        summed = lax.psum_scatter(partial_value, "col", scatter_dimension=1, tiled=True)
        own_source = lax.dynamic_index_in_dim(sources, cycle, 0, False)
        local_source = lax.dynamic_slice_in_dim(own_source, block_start, piece, 1)
        reduced = (local_source - summed).astype(jnp.bfloat16)
        term = jnp.dot(
            reduced,
            lax.dynamic_index_in_dim(inverse, cycle, 0, False),
            preferred_element_type=jnp.float32,
        )
        owner = index % n_row == my_row
        term = jnp.where(owner, term, 0.0)
        return lax.psum(term, ("row", "col"))

    empty_rows = jnp.zeros((slab, nrhs, width), jnp.float32)

    def left_step(index, solved):
        cycle = index // n_row
        own_row = cycle * n_row + my_row
        picked = lax.dynamic_index_in_dim(
            solved.reshape(per_col, n_col, nrhs, width), my_col, 1, False
        )
        rounded = picked.astype(jnp.bfloat16)
        limit = jnp.where(
            column_ids < own_row, lax.dynamic_index_in_dim(limits, cycle, 0, False), 0
        )
        terms = project(
            lax.dynamic_index_in_dim(v_tiles, cycle, 0, False),
            lax.dynamic_index_in_dim(u_tiles, cycle, 0, False),
            rounded,
            limit,
        )
        result = finish(jnp.sum(terms, axis=0), cycle, index)
        return lax.dynamic_update_index_in_dim(solved, result, index, 0)

    solved = lax.fori_loop(0, slab, left_step, empty_rows)
    square_block = lax.dynamic_slice_in_dim(inverse, block_start, piece, 2)
    diagonal = jnp.diagonal(square_block, axis1=1, axis2=2).astype(jnp.float32)
    log_sums = jnp.sum(jnp.log(diagonal), axis=1)
    logdiag = lax.psum(log_sums, "col") / width
    own_rows = lax.dynamic_index_in_dim(solved.reshape(cycles, n_row, nrhs, width), my_row, 1, True)
    quadratic = jnp.mean(own_rows * own_rows, axis=3)
    loglik = -0.5 * quadratic + logdiag[:, None, None] - 0.5 * math.log(2.0 * math.pi)
    return (own_rows, loglik)


def solution(mesh):
    placed = (
        P(None, "row", None, None),
        P(None, "row", "col", None),
        P(None, "row", None, "col", None, None),
        P(None, "row", None, "col", None, None),
        P(None, "row", None, "col"),
    )
    return jax.shard_map(
        local,
        mesh=mesh,
        in_specs=placed,
        out_specs=(P(None, "row", None, None), P(None, "row", None)),
        check_vma=False,
    )
```

profile of v0, /device:TPU:25, one launch (start us, length us, event | category | flops | bytes accessed | tf_op | source)
XLA Modules:
  0.0 587.5 jit_solution(18435897087358040744)
XLA Ops:
  7.2 0.7 copy-done
  7.9 0.6 copy-done.2
  8.5 557.8 %while.16 = (s32[]{:T(128)}, f32[8,4,1024]{2,1,0:T(4,128)S(1)}, s32[]{:T(128)}, f32[1,4,256]{2,1,0:T(4,128)S(1)}, s32[1,2]{1,0:T(1,128)S(1)}, /*index=5*/s32[]{:...) while((s32[]{:T(128)}, f32[8,4,1024]{2,1,0:T(4,128)S(1)}, ...), condition=%wide.region_3.4_spmd.clone, body=%wide.region_0.3_spmd.clone.sunk | while | flops 6304025 | bytes 4498590 | solution.py:76
  8.6 0.1 iota_compare_fusion.2
  8.6 2.5 convolution_bitcast_fusion.2
  11.2 26.7 %reduce-scatter.6.cloned.1.call-done = f32[256,4]{1,0:T(8,128)} async-done(((f32[1024,4]{1,0:T(8,128)}), f32[256,4]{1,0:T(8,128)}) %reduce-scatter.6.cloned.1.call-update) | async-done | bytes 4112 | tf_op jit(solution)/shard_map/while
  37.9 1.0 copy.12
  38.9 0.2 fusion.30
  39.1 37.8 %psum.24 = f32[1,4,1024]{2,1,0:T(4,128)S(1)} all-reduce(f32[1,4,1024]{2,1,0:T(4,128)S(1)} %fusion.30), channel_id=1, replica_groups=mesh['row'=8,'col'=4] {'row','col'}, use_global_device_ids=true, to_apply=%region_2.2 | all-reduce | flops 4096 | bytes 32768 | tf_op jit(solution)/shard_map/while/body/eval_jaxpr/psum | solution.py:53
  76.9 0.0 reduce-scatter.6.cloned.1.call-start
  77.0 0.1 iota_compare_fusion.2
  77.1 2.5 convolution_bitcast_fusion.2
  79.6 28.3 %reduce-scatter.6.cloned.1.call-done = f32[256,4]{1,0:T(8,128)} async-done(((f32[1024,4]{1,0:T(8,128)}), f32[256,4]{1,0:T(8,128)}) %reduce-scatter.6.cloned.1.call-update) | async-done | bytes 4112 | tf_op jit(solution)/shard_map/while
  107.9 1.0 copy.12
  108.9 0.2 fusion.30
  109.1 37.8 %psum.24 = f32[1,4,1024]{2,1,0:T(4,128)S(1)} all-reduce(f32[1,4,1024]{2,1,0:T(4,128)S(1)} %fusion.30), channel_id=1, replica_groups=mesh['row'=8,'col'=4] {'row','col'}, use_global_device_ids=true, to_apply=%region_2.2 | all-reduce | flops 4096 | bytes 32768 | tf_op jit(solution)/shard_map/while/body/eval_jaxpr/psum | solution.py:53
  146.9 0.0 reduce-scatter.6.cloned.1.call-start
  147.0 0.1 iota_compare_fusion.2
  147.1 2.5 convolution_bitcast_fusion.2
  149.6 28.3 %reduce-scatter.6.cloned.1.call-done = f32[256,4]{1,0:T(8,128)} async-done(((f32[1024,4]{1,0:T(8,128)}), f32[256,4]{1,0:T(8,128)}) %reduce-scatter.6.cloned.1.call-update) | async-done | bytes 4112 | tf_op jit(solution)/shard_map/while
  178.0 1.0 copy.12
  178.9 0.2 fusion.30
  179.1 37.8 %psum.24 = f32[1,4,1024]{2,1,0:T(4,128)S(1)} all-reduce(f32[1,4,1024]{2,1,0:T(4,128)S(1)} %fusion.30), channel_id=1, replica_groups=mesh['row'=8,'col'=4] {'row','col'}, use_global_device_ids=true, to_apply=%region_2.2 | all-reduce | flops 4096 | bytes 32768 | tf_op jit(solution)/shard_map/while/body/eval_jaxpr/psum | solution.py:53
  217.0 0.0 reduce-scatter.6.cloned.1.call-start
  217.0 0.1 iota_compare_fusion.2
  217.1 2.5 convolution_bitcast_fusion.2
  219.6 28.0 %reduce-scatter.6.cloned.1.call-done = f32[256,4]{1,0:T(8,128)} async-done(((f32[1024,4]{1,0:T(8,128)}), f32[256,4]{1,0:T(8,128)}) %reduce-scatter.6.cloned.1.call-update) | async-done | bytes 4112 | tf_op jit(solution)/shard_map/while
  247.7 1.0 copy.12
  248.7 0.2 fusion.30
  248.8 37.8 %psum.24 = f32[1,4,1024]{2,1,0:T(4,128)S(1)} all-reduce(f32[1,4,1024]{2,1,0:T(4,128)S(1)} %fusion.30), channel_id=1, replica_groups=mesh['row'=8,'col'=4] {'row','col'}, use_global_device_ids=true, to_apply=%region_2.2 | all-reduce | flops 4096 | bytes 32768 | tf_op jit(solution)/shard_map/while/body/eval_jaxpr/psum | solution.py:53
  286.7 0.0 reduce-scatter.6.cloned.1.call-start
  286.7 0.1 iota_compare_fusion.2
  286.8 2.5 convolution_bitcast_fusion.2
  289.4 28.1 %reduce-scatter.6.cloned.1.call-done = f32[256,4]{1,0:T(8,128)} async-done(((f32[1024,4]{1,0:T(8,128)}), f32[256,4]{1,0:T(8,128)}) %reduce-scatter.6.cloned.1.call-update) | async-done | bytes 4112 | tf_op jit(solution)/shard_map/while
  317.4 1.0 copy.12
  318.4 0.2 fusion.30
  318.6 37.8 %psum.24 = f32[1,4,1024]{2,1,0:T(4,128)S(1)} all-reduce(f32[1,4,1024]{2,1,0:T(4,128)S(1)} %fusion.30), channel_id=1, replica_groups=mesh['row'=8,'col'=4] {'row','col'}, use_global_device_ids=true, to_apply=%region_2.2 | all-reduce | flops 4096 | bytes 32768 | tf_op jit(solution)/shard_map/while/body/eval_jaxpr/psum | solution.py:53
  356.4 0.0 reduce-scatter.6.cloned.1.call-start
  356.5 0.1 iota_compare_fusion.2
  356.6 2.5 convolution_bitcast_fusion.2
  359.1 28.0 %reduce-scatter.6.cloned.1.call-done = f32[256,4]{1,0:T(8,128)} async-done(((f32[1024,4]{1,0:T(8,128)}), f32[256,4]{1,0:T(8,128)}) %reduce-scatter.6.cloned.1.call-update) | async-done | bytes 4112 | tf_op jit(solution)/shard_map/while
  387.1 1.0 copy.12
  388.1 0.2 fusion.30
  388.3 37.8 %psum.24 = f32[1,4,1024]{2,1,0:T(4,128)S(1)} all-reduce(f32[1,4,1024]{2,1,0:T(4,128)S(1)} %fusion.30), channel_id=1, replica_groups=mesh['row'=8,'col'=4] {'row','col'}, use_global_device_ids=true, to_apply=%region_2.2 | all-reduce | flops 4096 | bytes 32768 | tf_op jit(solution)/shard_map/while/body/eval_jaxpr/psum | solution.py:53
  426.2 0.0 reduce-scatter.6.cloned.1.call-start
  426.2 0.1 iota_compare_fusion.2
  426.3 2.5 convolution_bitcast_fusion.2
  428.9 28.4 %reduce-scatter.6.cloned.1.call-done = f32[256,4]{1,0:T(8,128)} async-done(((f32[1024,4]{1,0:T(8,128)}), f32[256,4]{1,0:T(8,128)}) %reduce-scatter.6.cloned.1.call-update) | async-done | bytes 4112 | tf_op jit(solution)/shard_map/while
  457.3 1.0 copy.12
  458.2 0.2 fusion.30
  458.4 37.8 %psum.24 = f32[1,4,1024]{2,1,0:T(4,128)S(1)} all-reduce(f32[1,4,1024]{2,1,0:T(4,128)S(1)} %fusion.30), channel_id=1, replica_groups=mesh['row'=8,'col'=4] {'row','col'}, use_global_device_ids=true, to_apply=%region_2.2 | all-reduce | flops 4096 | bytes 32768 | tf_op jit(solution)/shard_map/while/body/eval_jaxpr/psum | solution.py:53
  496.3 0.0 reduce-scatter.6.cloned.1.call-start
  496.3 0.1 iota_compare_fusion.2
  496.4 2.5 convolution_bitcast_fusion.2
  498.9 28.4 %reduce-scatter.6.cloned.1.call-done = f32[256,4]{1,0:T(8,128)} async-done(((f32[1024,4]{1,0:T(8,128)}), f32[256,4]{1,0:T(8,128)}) %reduce-scatter.6.cloned.1.call-update) | async-done | bytes 4112 | tf_op jit(solution)/shard_map/while
  527.4 1.0 copy.12
  528.3 0.2 fusion.30
  528.5 37.8 %psum.24 = f32[1,4,1024]{2,1,0:T(4,128)S(1)} all-reduce(f32[1,4,1024]{2,1,0:T(4,128)S(1)} %fusion.30), channel_id=1, replica_groups=mesh['row'=8,'col'=4] {'row','col'}, use_global_device_ids=true, to_apply=%region_2.2 | all-reduce | flops 4096 | bytes 32768 | tf_op jit(solution)/shard_map/while/body/eval_jaxpr/psum | solution.py:53
  566.3 0.7 multiply_reduce_fusion
  567.1 0.9 dynamic-slice_bitcast_fusion
  568.0 2.5 gather_fusion
  570.5 0.6 log_reduce_fusion
  571.1 8.4 %psum.21 = f32[1]{0:T(128)} all-reduce(f32[1]{0:T(128)} %bitcast.8), channel_id=1, replica_groups=mesh['row'=8,'col'=4] {'col'}, use_global_device_ids=true, to_apply=%region_6.7 | all-reduce | flops 1 | bytes 8 | tf_op jit(solution)/shard_map/psum | solution.py:80
  580.1 0.5 add_bitcast_fusion
  (46 shorter events, 0.4 us)
Async XLA Ops:
  7.2 0.7 copy-start
  7.9 0.7 copy-start.2
  8.5 29.4 %reduce-scatter.6.cloned.1.call-start = ((), (), s32[]{:S(2)}) async-start(), calls=%async_computation.1 | async-start | bytes 655360 | tf_op jit(solution)/shard_map/while
  11.1 27.7 %copy-start.1 = (bf16[1,256,1024]{2,1,0:T(8,128)(2,1)S(1)}, bf16[1,256,1024]{2,1,0:T(8,128)(2,1)}, u32[]{:S(2)}) copy-start(bf16[1,256,1024]{2,1,0:T(8,128)(2,1)} %get-tuple-element.422) | copy-start | bytes 1572868 | tf_op jit(solution)/shard_map/while
  76.9 31.0 %reduce-scatter.6.cloned.1.call-start = ((), (), s32[]{:S(2)}) async-start(), calls=%async_computation.1 | async-start | bytes 655360 | tf_op jit(solution)/shard_map/while
  79.6 29.3 %copy-start.1 = (bf16[1,256,1024]{2,1,0:T(8,128)(2,1)S(1)}, bf16[1,256,1024]{2,1,0:T(8,128)(2,1)}, u32[]{:S(2)}) copy-start(bf16[1,256,1024]{2,1,0:T(8,128)(2,1)} %get-tuple-element.422) | copy-start | bytes 1572868 | tf_op jit(solution)/shard_map/while
  146.9 31.0 %reduce-scatter.6.cloned.1.call-start = ((), (), s32[]{:S(2)}) async-start(), calls=%async_computation.1 | async-start | bytes 655360 | tf_op jit(solution)/shard_map/while
  149.6 29.3 %copy-start.1 = (bf16[1,256,1024]{2,1,0:T(8,128)(2,1)S(1)}, bf16[1,256,1024]{2,1,0:T(8,128)(2,1)}, u32[]{:S(2)}) copy-start(bf16[1,256,1024]{2,1,0:T(8,128)(2,1)} %get-tuple-element.422) | copy-start | bytes 1572868 | tf_op jit(solution)/shard_map/while
  217.0 30.7 %reduce-scatter.6.cloned.1.call-start = ((), (), s32[]{:S(2)}) async-start(), calls=%async_computation.1 | async-start | bytes 655360 | tf_op jit(solution)/shard_map/while
  219.6 29.0 %copy-start.1 = (bf16[1,256,1024]{2,1,0:T(8,128)(2,1)S(1)}, bf16[1,256,1024]{2,1,0:T(8,128)(2,1)}, u32[]{:S(2)}) copy-start(bf16[1,256,1024]{2,1,0:T(8,128)(2,1)} %get-tuple-element.422) | copy-start | bytes 1572868 | tf_op jit(solution)/shard_map/while
  286.7 30.8 %reduce-scatter.6.cloned.1.call-start = ((), (), s32[]{:S(2)}) async-start(), calls=%async_computation.1 | async-start | bytes 655360 | tf_op jit(solution)/shard_map/while
  289.3 29.1 %copy-start.1 = (bf16[1,256,1024]{2,1,0:T(8,128)(2,1)S(1)}, bf16[1,256,1024]{2,1,0:T(8,128)(2,1)}, u32[]{:S(2)}) copy-start(bf16[1,256,1024]{2,1,0:T(8,128)(2,1)} %get-tuple-element.422) | copy-start | bytes 1572868 | tf_op jit(solution)/shard_map/while
  356.4 30.7 %reduce-scatter.6.cloned.1.call-start = ((), (), s32[]{:S(2)}) async-start(), calls=%async_computation.1 | async-start | bytes 655360 | tf_op jit(solution)/shard_map/while
  359.1 29.0 %copy-start.1 = (bf16[1,256,1024]{2,1,0:T(8,128)(2,1)S(1)}, bf16[1,256,1024]{2,1,0:T(8,128)(2,1)}, u32[]{:S(2)}) copy-start(bf16[1,256,1024]{2,1,0:T(8,128)(2,1)} %get-tuple-element.422) | copy-start | bytes 1572868 | tf_op jit(solution)/shard_map/while
  426.2 31.1 %reduce-scatter.6.cloned.1.call-start = ((), (), s32[]{:S(2)}) async-start(), calls=%async_computation.1 | async-start | bytes 655360 | tf_op jit(solution)/shard_map/while
  428.8 29.4 %copy-start.1 = (bf16[1,256,1024]{2,1,0:T(8,128)(2,1)S(1)}, bf16[1,256,1024]{2,1,0:T(8,128)(2,1)}, u32[]{:S(2)}) copy-start(bf16[1,256,1024]{2,1,0:T(8,128)(2,1)} %get-tuple-element.422) | copy-start | bytes 1572868 | tf_op jit(solution)/shard_map/while
  496.3 31.1 %reduce-scatter.6.cloned.1.call-start = ((), (), s32[]{:S(2)}) async-start(), calls=%async_computation.1 | async-start | bytes 655360 | tf_op jit(solution)/shard_map/while
  498.9 29.4 %copy-start.1 = (bf16[1,256,1024]{2,1,0:T(8,128)(2,1)S(1)}, bf16[1,256,1024]{2,1,0:T(8,128)(2,1)}, u32[]{:S(2)}) copy-start(bf16[1,256,1024]{2,1,0:T(8,128)(2,1)} %get-tuple-element.422) | copy-start | bytes 1572868 | tf_op jit(solution)/shard_map/while
Sparse Core Ops, SparseCore 0:
  12.2 25.6 reduce-scatter.5
  80.5 27.3 reduce-scatter.5
  150.6 27.3 reduce-scatter.5
  220.3 27.3 reduce-scatter.5
  290.0 27.4 reduce-scatter.5
  359.8 27.3 reduce-scatter.5
  429.8 27.4 reduce-scatter.5
  499.9 27.4 reduce-scatter.5
where the time goes:
time: 596 us; the launch traced here: 587 us
  blocking collectives  311 us (52%)
  waiting for transfers between devices  224 us (38%)
  matrix products  21.6 us (4%)
  between operations  14.7 us (2%)
  local copies, waits for them, and re-layouts  12.7 us (2%)
    psum x8, blocking collectives, finish(): return lax.psum(term, ('row', 'col'))  302 us
    while x16, waiting for transfers between devices  224 us
    dot_general x8, matrix products, rank_part(): jnp.einsum('brk,brn->bkn', inner, u_tiles, preferred_element_type=jnp.flo...  20 us
  transfers between devices with their start and end apart: 8, of which 8 were waited for; matrix products, arithmetic and copies ran while one was open for 0% of the time, Pallas kernels for 0%

commit v1 on v0

v1 whole, which is shorter than its diff:
```python
import functools
import math

import jax
import jax.numpy as jnp
from jax import lax
from jax.experimental import pallas as pl
from jax.experimental.pallas import tpu as pltpu
from jax.sharding import PartitionSpec as P

MESH = pl.DeviceIdType.MESH
NT = (((1,), (1,)), ((), ()))


def remote(src, dst, send_sem, recv_sem, device):
    return pltpu.make_async_remote_copy(
        src_ref=src,
        dst_ref=dst,
        send_sem=send_sem,
        recv_sem=recv_sem,
        device_id=device,
        device_id_type=MESH,
    )


def kernel(
    n_row, n_col,
    rhs_ref, inv_ref, u_ref, v_ref, rank_ref,
    white_ref, lik_ref,
    y_in, p_out, p_in, y_row, logs, base,
    y_send, y_recv, p_send, p_recv, o_send, o_recv, l_send, l_recv,
):
    row = lax.axis_index("row")
    col = lax.axis_index("col")
    per_col = u_ref.shape[2]
    rank_max = u_ref.shape[4]
    nrhs, width = rhs_ref.shape[2], rhs_ref.shape[3]
    piece = width // n_col
    peers = [lax.rem(col + k, n_col) for k in range(1, n_col)]
    own_slot = row // n_col
    own_home = lax.rem(row, n_col)

    barrier = pltpu.get_barrier_semaphore()
    for peer in peers:
        pl.semaphore_signal(barrier, inc=1, device_id=(row, peer), device_id_type=MESH)

    def greet_later(i, count):
        pl.semaphore_signal(barrier, inc=1, device_id=(i, own_home), device_id_type=MESH)
        return count + 1

    greeted = lax.fori_loop(row + 1, n_row, greet_later, n_col - 1)
    for q in range(per_col):
        j = q * n_col + col

        @pl.when(j < row)
        def _():
            for s in range(n_col):
                pl.semaphore_signal(barrier, inc=1, device_id=(j, s), device_id_type=MESH)

        greeted = greeted + jnp.where(j < row, n_col, 0)

    for cc in range(n_col):

        @pl.when(col == cc)
        def _():
            lo = cc * piece
            base[...] = rhs_ref[0, 0, :, lo:lo + piece]
            block = inv_ref[0, 0, :, lo:lo + piece].astype(jnp.float32)
            r_id = lax.broadcasted_iota(jnp.int32, (piece, piece), 0)
            c_id = lax.broadcasted_iota(jnp.int32, (piece, piece), 1)
            diagonal = jnp.sum(jnp.where(r_id == c_id, block, 0.0), axis=0, keepdims=True)
            total = jnp.sum(jnp.log(diagonal), axis=1, keepdims=True)
            logs[cc] = jnp.broadcast_to(total, (1, 128))

    pl.semaphore_wait(barrier, greeted)

    for k, peer in enumerate(peers):
        remote(logs.at[col], logs.at[col], l_send.at[k], l_recv.at[col], (row, peer)).start()

    for q in range(per_col):
        j = q * n_col + col

        @pl.when(j < row)
        def _():
            for s in range(n_col):
                remote(y_in.at[q, s], y_in.at[q, s], y_send.at[0], y_recv.at[q, s], (j, s)).wait_recv()
            y = y_in[q, 0]
            for s in range(1, n_col):
                y = y + y_in[q, s]
            inner = lax.dot_general(y.astype(jnp.bfloat16), v_ref[0, 0, q, 0], NT, preferred_element_type=jnp.float32)
            keep = lax.broadcasted_iota(jnp.int32, (nrhs, rank_max), 1) < rank_ref[0, 0, q, 0]
            inner = jnp.where(keep, inner, 0.0).astype(jnp.bfloat16)
            p = jnp.dot(inner, u_ref[0, 0, q, 0], preferred_element_type=jnp.float32)
            for s in range(n_col):
                p_out[q, s] = p[:, s * piece:(s + 1) * piece]
            for k, peer in enumerate(peers):
                remote(p_out.at[q, peer], p_in.at[j], p_send.at[q, k], p_recv.at[j], (row, peer)).start()
            p_in[j] = p_out[q, col]

    def gather_p(j, acc):
        home = lax.rem(j, n_col)

        @pl.when(home != col)
        def _():
            remote(p_in.at[j], p_in.at[j], p_send.at[0, 0], p_recv.at[j], (row, home)).wait_recv()

        return acc + p_in[j]

    total = lax.fori_loop(0, row, gather_p, jnp.zeros((nrhs, piece), jnp.float32))
    reduced = (base[...] - total).astype(jnp.bfloat16)
    y_row[col] = jnp.dot(reduced, inv_ref[0, 0], preferred_element_type=jnp.float32)

    def send_y(i, carry):
        remote(y_row.at[col], y_in.at[own_slot, col], y_send.at[i], y_recv.at[own_slot, col], (i, own_home)).start()
        return carry

    lax.fori_loop(row + 1, n_row, send_y, 0)
    for k, peer in enumerate(peers):
        remote(y_row.at[col], y_row.at[col], o_send.at[k], o_recv.at[col], (row, peer)).start()
    for k, peer in enumerate(peers):
        remote(logs.at[peer], logs.at[peer], l_send.at[k], l_recv.at[peer], (row, peer)).wait_recv()
        remote(y_row.at[peer], y_row.at[peer], o_send.at[k], o_recv.at[peer], (row, peer)).wait_recv()
    y = y_row[0]
    log_sum = logs[0]
    for s in range(1, n_col):
        y = y + y_row[s]
        log_sum = log_sum + logs[s]
    white_ref[0, 0] = y
    quadratic = jnp.sum(y * y, axis=1, keepdims=True) * (1.0 / width)
    lik = -0.5 * quadratic + log_sum * (1.0 / width) - 0.5 * math.log(2.0 * math.pi)
    r_id = lax.broadcasted_iota(jnp.int32, (nrhs, 128), 0)
    c_id = lax.broadcasted_iota(jnp.int32, (nrhs, 128), 1)
    flat = jnp.sum(jnp.where(r_id == c_id, lik, 0.0), axis=0, keepdims=True)
    lik_ref[0] = flat[:, :nrhs]

    def left_y(i, carry):
        remote(y_row.at[col], y_in.at[own_slot, col], y_send.at[i], y_recv.at[own_slot, col], (i, own_home)).wait_send()
        return carry

    lax.fori_loop(row + 1, n_row, left_y, 0)
    for k, peer in enumerate(peers):
        remote(logs.at[col], logs.at[col], l_send.at[k], l_recv.at[col], (row, peer)).wait_send()
        remote(y_row.at[col], y_row.at[col], o_send.at[k], o_recv.at[col], (row, peer)).wait_send()
    for q in range(per_col):
        j = q * n_col + col

        @pl.when(j < row)
        def _():
            for k, peer in enumerate(peers):
                remote(p_out.at[q, peer], p_in.at[j], p_send.at[q, k], p_recv.at[j], (row, peer)).wait_send()


def local(n_row, n_col, right_side, inverse_t, u_factor, v_factor, ranks):
    nrhs, width = right_side.shape[2:]
    per_col = u_factor.shape[2]
    piece = width // n_col
    vmem = pl.BlockSpec(memory_space=pltpu.VMEM)
    dma = pltpu.SemaphoreType.DMA
    return pl.pallas_call(
        functools.partial(kernel, n_row, n_col),
        out_shape=(
            jax.ShapeDtypeStruct((1, 1, nrhs, width), jnp.float32),
            jax.ShapeDtypeStruct((1, 1, nrhs), jnp.float32),
        ),
        in_specs=[vmem, vmem, vmem, vmem, pl.BlockSpec(memory_space=pltpu.SMEM)],
        out_specs=(vmem, vmem),
        scratch_shapes=[
            pltpu.VMEM((per_col, n_col, nrhs, width), jnp.float32),
            pltpu.VMEM((per_col, n_col, nrhs, piece), jnp.float32),
            pltpu.VMEM((n_row, nrhs, piece), jnp.float32),
            pltpu.VMEM((n_col, nrhs, width), jnp.float32),
            pltpu.VMEM((n_col, 1, 128), jnp.float32),
            pltpu.VMEM((nrhs, piece), jnp.float32),
            dma((n_row,)),
            dma((per_col, n_col)),
            dma((per_col, n_col)),
            dma((n_row,)),
            dma((n_col,)),
            dma((n_col,)),
            dma((n_col,)),
            dma((n_col,)),
        ],
        compiler_params=pltpu.CompilerParams(collective_id=0, has_side_effects=True),
        name="forward_solve",
    )(right_side, inverse_t, u_factor, v_factor, ranks)


def solution(mesh):
    placed = (
        P(None, "row", None, None),
        P(None, "row", "col", None),
        P(None, "row", None, "col", None, None),
        P(None, "row", None, "col", None, None),
        P(None, "row", None, "col"),
    )
    return jax.shard_map(
        functools.partial(local, mesh.shape["row"], mesh.shape["col"]),
        mesh=mesh,
        in_specs=placed,
        out_specs=(P(None, "row", None, None), P(None, "row", None)),
        check_vma=False,
    )
```

time: 596 us -> 51.2 us (0.09); the launches traced: 587 us -> 51 us
  blocking collectives: 311 us -> 0 us
  waiting for transfers between devices: 224 us -> 0 us
  Pallas kernels: 0 us -> 47.2 us
  matrix products: 21.6 us -> 0 us
  between operations: 14.7 us -> 0.65 us
  local copies, waits for them, and re-layouts: 12.7 us -> 3.14 us
    psum x9 -> x0, blocking collectives: 311 us -> none  [the longest x8 302 us: finish(): return lax.psum(term, ('row', 'col'))]
    while x16 -> x0, waiting for transfers between devices: 224 us -> none
    pallas_call x0 -> x1, Pallas kernels: none -> 47.2 us  [local(): pl.pallas_call(functools.partial(kernel, n_row, n_col), out_shape=(jax.Sh...]
    dot_general x16 -> x0, matrix products: 21.6 us -> none  [the longest x8 20 us: rank_part(): jnp.einsum('brk,brn->bkn', inner, u_tiles, preferred_element_type=jnp.flo...]
    while x24 -> x0, local copies, waits for them, and re-layouts: 7.84 us -> none
  transfers between devices with their start and end apart: 8 -> 0, of which waited for: 8 -> 0; matrix products, arithmetic and copies ran while one was open for 0% -> 0% of each run, Pallas kernels for 0% -> 0%
where the time goes in v1:
time: 51.2 us; the launch traced here: 51 us
  Pallas kernels  47.2 us (92%)
  local copies, waits for them, and re-layouts  3.14 us (6%)
  between operations  0.65 us (1%)
    pallas_call x1, Pallas kernels, local(): pl.pallas_call(functools.partial(kernel, n_row, n_col), out_shape=(jax.Sh...  47.2 us
    unnamed x5, local copies, waits for them, and re-layouts  3.14 us

profile of v1, /device:TPU:25, one launch (start us, length us, event | category | flops | bytes accessed | tf_op | source)
XLA Modules:
  0.0 51.0 jit_solution(16183611644722997394)
XLA Ops:
  0.6 1.3 %copy.7.rank_ref = s32[1,1,2,1]{3,2,1,0:T(2,128)} copy(s32[1,1,2,1]{2,3,1,0:T(1,128)} %param.9) | data formatting | bytes 16 | tf_op args[4]
  1.9 47.2 %forward_solve.1 = (f32[1,1,4,1024]{3,2,1,0:T(4,128)}, f32[1,1,4]{2,1,0:T(1,128)}) custom-call(f32[1,1,4,1024]{3,2,1,0:T(4,128)} %rhs_ref.1, bf16[1,1,256,1024]{3,2,1,0:T(8,128)(2,1)} %inv_ref.1, bf16[1,1,2,1,128,1024]{5,4,3,2,1,0:T(8,128)(2,1)} %u_ref.1, bf16[1,1,2,1,128,1024]{5,4,3,2,1,0:T(8,128)(2,1)} %v_ref.1, s32[1,1,2,1]{3,2,1,0:T(2,128)} %copy.7.rank_ref), custom_call_target="tpu_custom_call" | custom-call | tf_op jit(solution)/shard_map/forward_solve/pallas_call | solution.py:159
  49.1 0.0 copy-start
  49.1 1.3 %copy.10 = f32[1,1,4,1024]{3,2,1,0:T(4,128)} copy(f32[1,1,4,1024]{3,2,1,0:T(4,128)} %get-tuple-element.4) | data formatting | bytes 32768
  50.5 0.0 copy-done
  50.5 0.5 %copy.11 = f32[1,1,4]{2,1,0:T(1,128)} copy(f32[1,1,4]{2,1,0:T(1,128)S(1)} %copy-done) | data formatting | bytes 32
Async XLA Ops:
  49.1 1.3 %copy-start = (f32[1,1,4]{2,1,0:T(1,128)S(1)}, f32[1,1,4]{2,1,0:T(1,128)}, u32[]{:S(2)}) copy-start(f32[1,1,4]{2,1,0:T(1,128)} %get-tuple-element.5) | copy-start | bytes 52

commit v2 on v1

v2 whole, which is shorter than its diff:
```python
import functools
import math

import jax
import jax.numpy as jnp
from jax import lax
from jax.experimental import pallas as pl
from jax.experimental.pallas import tpu as pltpu
from jax.sharding import PartitionSpec as P

MESH = pl.DeviceIdType.MESH
NT = (((1,), (1,)), ((), ()))


def remote(src, dst, send_sem, recv_sem, device):
    return pltpu.make_async_remote_copy(
        src_ref=src,
        dst_ref=dst,
        send_sem=send_sem,
        recv_sem=recv_sem,
        device_id=device,
        device_id_type=MESH,
    )


def kernel(
    n_row, n_col,
    rhs_hbm, inv_hbm, u_hbm, v_hbm, rank_ref,
    white_ref, lik_ref,
    rhs_ref, inv_ref, u_ref, v_ref,
    y_in, p_out, p_in, y_row, logs, base,
    v_out, v_in, u_out, u_in, fold, w_out, w_in,
    in_sem, y_send, y_recv, p_send, p_recv, o_send, o_recv, l_send, l_recv,
    v_send, v_recv, u_send, u_recv, w_send, w_recv,
):
    row = lax.axis_index("row")
    col = lax.axis_index("col")
    per_col, rank_max, width = u_ref.shape
    nrhs = rhs_ref.shape[0]
    piece = width // n_col
    peers = [lax.rem(col + k, n_col) for k in range(1, n_col)]
    own_slot = row // n_col
    own_home = lax.rem(row, n_col)
    last = n_row - 1

    copies = [
        pltpu.make_async_copy(v_hbm.at[0, 0, :, 0], v_ref, in_sem.at[0]),
        pltpu.make_async_copy(u_hbm.at[0, 0, :, 0], u_ref, in_sem.at[1]),
        pltpu.make_async_copy(inv_hbm.at[0, 0], inv_ref, in_sem.at[2]),
        pltpu.make_async_copy(rhs_hbm.at[0, 0], rhs_ref, in_sem.at[3]),
    ]
    for copy in copies:
        copy.start()

    short = row >= 2
    feeds = (row >= 1) & (row < last)
    long_count = jnp.where(short, row - 1, row)
    long_first = jnp.where(row == 0, 1, row + 2)

    barrier = pltpu.get_barrier_semaphore()

    def greet(i, s):
        pl.semaphore_signal(barrier, inc=1, device_id=(i, s), device_id_type=MESH)

    for peer in peers:
        greet(row, peer)
    greeted = jnp.int32(n_col - 1)

    @pl.when(row < last)
    def _():
        for s in range(n_col):
            greet(row + 1, s)

    greeted = greeted + jnp.where(row < last, n_col, 0)

    @pl.when(row > 0)
    def _():
        for s in range(n_col):
            greet(row - 1, s)

    greeted = greeted + jnp.where(row > 0, n_col, 0)

    def greet_later(i, count):
        greet(i, own_home)
        return count + 1

    greeted = lax.fori_loop(row + 2, n_row, greet_later, greeted)
    for q in range(per_col):
        j = q * n_col + col

        @pl.when(j < row - 1)
        def _():
            for s in range(n_col):
                greet(j, s)

        greeted = greeted + jnp.where(j < row - 1, n_col, 0)

    prev_slot = jnp.maximum(row - 1, 0) // n_col
    prev_home = lax.rem(jnp.maximum(row - 1, 0), n_col)
    gives = short & (col == prev_home)
    copies[0].wait()
    copies[1].wait()

    @pl.when(gives)
    def _():
        v_tile = v_ref[prev_slot].astype(jnp.float32)
        keep = lax.broadcasted_iota(jnp.int32, (rank_max, width), 0) < rank_ref[prev_slot]
        u_tile = jnp.where(keep, u_ref[prev_slot].astype(jnp.float32), 0.0)
        for s in range(n_col):
            v_out[s] = v_tile[:, s * piece:(s + 1) * piece]
            u_out[s] = u_tile[:, s * piece:(s + 1) * piece]

    pl.semaphore_wait(barrier, greeted)

    def v_copy(s, i):
        part = pl.ds(s, n_col - s)
        return remote(v_out.at[part], v_in.at[part], v_send.at[s], v_recv, (i, s))

    def u_copy(k, peer):
        return remote(u_out.at[peer], u_in, u_send.at[k], u_recv, (row, peer))

    @pl.when(gives)
    def _():
        for s in range(n_col):
            v_copy(s, row - 1).start()
        for k, peer in enumerate(peers):
            u_copy(k, peer).start()
        u_in[...] = u_out[col]

    copies[2].wait()
    copies[3].wait()

    for cc in range(n_col):

        @pl.when(col == cc)
        def _():
            base[...] = rhs_ref[:, cc * piece:(cc + 1) * piece]

    def log_part():
        for cc in range(n_col):

            @pl.when(col == cc)
            def _():
                block = inv_ref[:, cc * piece:(cc + 1) * piece].astype(jnp.float32)
                r_id = lax.broadcasted_iota(jnp.int32, (piece, piece), 0)
                c_id = lax.broadcasted_iota(jnp.int32, (piece, piece), 1)
                diagonal = jnp.sum(jnp.where(r_id == c_id, block, 0.0), axis=0, keepdims=True)
                total = jnp.sum(jnp.log(diagonal), axis=1, keepdims=True)
                logs[cc] = jnp.broadcast_to(total, (1, 128))

        for k, peer in enumerate(peers):
            remote(logs.at[col], logs.at[col], l_send.at[k], l_recv.at[col], (row, peer)).start()

    pl.when(row > 0)(log_part)

    for q in range(per_col):
        j = q * n_col + col

        @pl.when(j < long_count)
        def _():
            for s in range(n_col):
                remote(y_in.at[q, s], y_in.at[q, s], y_send.at[0], y_recv.at[q, s], (j, s)).wait_recv()
            y = y_in[q, 0]
            for s in range(1, n_col):
                y = y + y_in[q, s]
            inner = lax.dot_general(y.astype(jnp.bfloat16), v_ref[q], NT, preferred_element_type=jnp.float32)
            keep = lax.broadcasted_iota(jnp.int32, (nrhs, rank_max), 1) < rank_ref[q]
            inner = jnp.where(keep, inner, 0.0).astype(jnp.bfloat16)
            p = jnp.dot(inner, u_ref[q], preferred_element_type=jnp.float32)
            for s in range(n_col):
                p_out[q, s] = p[:, s * piece:(s + 1) * piece]
            for k, peer in enumerate(peers):
                remote(p_out.at[q, peer], p_in.at[j], p_send.at[q, k], p_recv.at[j], (row, peer)).start()
            p_in[j] = p_out[q, col]

    @pl.when(feeds)
    def _():
        fold[...] = jnp.zeros_like(fold)
        for cc in range(n_col):

            @pl.when(col == cc)
            def _():
                v_copy(cc, row).wait_recv()

        for cc in range(n_col):

            @pl.when(col <= cc)
            def _():
                part = lax.dot_general(
                    inv_ref[:, cc * piece:(cc + 1) * piece],
                    v_in[cc].astype(jnp.bfloat16),
                    NT,
                    preferred_element_type=jnp.float32,
                )
                fold[...] += part

    def gather_p(j, acc):
        home = lax.rem(j, n_col)

        @pl.when(home != col)
        def _():
            remote(p_in.at[j], p_in.at[j], p_send.at[0, 0], p_recv.at[j], (row, home)).wait_recv()

        return acc - p_in[j]

    base[...] = lax.fori_loop(0, long_count, gather_p, base[...])

    @pl.when(short)
    def _():
        @pl.when(col != prev_home)
        def _():
            remote(u_in, u_in, u_send.at[0], u_recv, (row, prev_home)).wait_recv()

        u_part = u_in[...].astype(jnp.bfloat16)
        for s in range(n_col):
            remote(w_in.at[s], w_in.at[s], w_send.at[0], w_recv.at[s], (row - 1, s)).wait_recv()
        inner = w_in[0]
        for s in range(1, n_col):
            inner = inner + w_in[s]
        base[...] -= jnp.dot(inner.astype(jnp.bfloat16), u_part, preferred_element_type=jnp.float32)

    reduced = base[...].astype(jnp.bfloat16)

    @pl.when(feeds)
    def _():
        w_out[...] = jnp.dot(reduced, fold[...].astype(jnp.bfloat16), preferred_element_type=jnp.float32)
        for s in range(n_col):
            remote(w_out, w_in.at[col], w_send.at[s], w_recv.at[col], (row + 1, s)).start()

    y_row[col] = jnp.dot(reduced, inv_ref[...], preferred_element_type=jnp.float32)

    def send_y(i, carry):
        remote(y_row.at[col], y_in.at[own_slot, col], y_send.at[i], y_recv.at[own_slot, col], (i, own_home)).start()
        return carry

    lax.fori_loop(long_first, n_row, send_y, 0)
    for k, peer in enumerate(peers):
        remote(y_row.at[col], y_row.at[col], o_send.at[k], o_recv.at[col], (row, peer)).start()
    pl.when(row == 0)(log_part)
    for k, peer in enumerate(peers):
        remote(logs.at[peer], logs.at[peer], l_send.at[k], l_recv.at[peer], (row, peer)).wait_recv()
        remote(y_row.at[peer], y_row.at[peer], o_send.at[k], o_recv.at[peer], (row, peer)).wait_recv()
    y = y_row[0]
    log_sum = logs[0]
    for s in range(1, n_col):
        y = y + y_row[s]
        log_sum = log_sum + logs[s]
    white_ref[0, 0] = y
    quadratic = jnp.sum(y * y, axis=1, keepdims=True) * (1.0 / width)
    lik = -0.5 * quadratic + log_sum * (1.0 / width) - 0.5 * math.log(2.0 * math.pi)
    r_id = lax.broadcasted_iota(jnp.int32, (nrhs, 128), 0)
    c_id = lax.broadcasted_iota(jnp.int32, (nrhs, 128), 1)
    flat = jnp.sum(jnp.where(r_id == c_id, lik, 0.0), axis=0, keepdims=True)
    lik_ref[0] = flat[:, :nrhs]

    def left_y(i, carry):
        remote(y_row.at[col], y_in.at[own_slot, col], y_send.at[i], y_recv.at[own_slot, col], (i, own_home)).wait_send()
        return carry

    lax.fori_loop(long_first, n_row, left_y, 0)
    for k, peer in enumerate(peers):
        remote(logs.at[col], logs.at[col], l_send.at[k], l_recv.at[col], (row, peer)).wait_send()
        remote(y_row.at[col], y_row.at[col], o_send.at[k], o_recv.at[col], (row, peer)).wait_send()

    @pl.when(feeds)
    def _():
        for s in range(n_col):
            remote(w_out, w_in.at[col], w_send.at[s], w_recv.at[col], (row + 1, s)).wait_send()

    @pl.when(gives)
    def _():
        for s in range(n_col):
            v_copy(s, row - 1).wait_send()
        for k, peer in enumerate(peers):
            u_copy(k, peer).wait_send()

    for q in range(per_col):
        j = q * n_col + col

        @pl.when(j < long_count)
        def _():
            for k, peer in enumerate(peers):
                remote(p_out.at[q, peer], p_in.at[j], p_send.at[q, k], p_recv.at[j], (row, peer)).wait_send()


def local(n_row, n_col, right_side, inverse_t, u_factor, v_factor, ranks):
    nrhs, width = right_side.shape[2:]
    per_col, _, rank_max = u_factor.shape[2:5]
    piece = width // n_col
    vmem = pl.BlockSpec(memory_space=pltpu.VMEM)
    hbm = pl.BlockSpec(memory_space=pl.ANY)
    dma = pltpu.SemaphoreType.DMA

    def f32(*shape):
        return pltpu.VMEM(shape, jnp.float32)

    def bf16(*shape):
        return pltpu.VMEM(shape, jnp.bfloat16)

    return pl.pallas_call(
        functools.partial(kernel, n_row, n_col),
        out_shape=(
            jax.ShapeDtypeStruct((1, 1, nrhs, width), jnp.float32),
            jax.ShapeDtypeStruct((1, 1, nrhs), jnp.float32),
        ),
        in_specs=[hbm, hbm, hbm, hbm, pl.BlockSpec(memory_space=pltpu.SMEM)],
        out_specs=(vmem, vmem),
        scratch_shapes=[
            f32(nrhs, width),
            bf16(piece, width),
            bf16(per_col, rank_max, width),
            bf16(per_col, rank_max, width),
            f32(per_col, n_col, nrhs, width),
            f32(per_col, n_col, nrhs, piece),
            f32(n_row, nrhs, piece),
            f32(n_col, nrhs, width),
            f32(n_col, 1, 128),
            f32(nrhs, piece),
            f32(n_col, rank_max, piece),
            f32(n_col, rank_max, piece),
            f32(n_col, rank_max, piece),
            f32(rank_max, piece),
            f32(piece, rank_max),
            f32(nrhs, rank_max),
            f32(n_col, nrhs, rank_max),
            dma((4,)),
            dma((n_row,)),
            dma((per_col, n_col)),
            dma((per_col, n_col)),
            dma((n_row,)),
            dma((n_col,)),
            dma((n_col,)),
            dma((n_col,)),
            dma((n_col,)),
            dma((n_col,)),
            dma,
            dma((n_col,)),
            dma,
            dma((n_col,)),
            dma((n_col,)),
        ],
        compiler_params=pltpu.CompilerParams(collective_id=0, has_side_effects=True),
        name="forward_solve",
    )(right_side, inverse_t, u_factor, v_factor, ranks.reshape(per_col))


def solution(mesh):
    placed = (
        P(None, "row", None, None),
        P(None, "row", "col", None),
        P(None, "row", None, "col", None, None),
        P(None, "row", None, "col", None, None),
        P(None, "row", None, "col"),
    )
    return jax.shard_map(
        functools.partial(local, mesh.shape["row"], mesh.shape["col"]),
        mesh=mesh,
        in_specs=placed,
        out_specs=(P(None, "row", None, None), P(None, "row", None)),
        check_vma=False,
    )
```

time: 51.2 us -> 47.6 us (0.930)
  Pallas kernels: 47.2 us -> 45 us
  local copies, waits for them, and re-layouts: 3.14 us -> 1.84 us
    pallas_call x1, Pallas kernels: 47.2 us -> 45 us  [local(): pl.pallas_call(functools.partial(kernel, n_row, n_col), out_shape=(jax.Sh...]
    unnamed x5 -> x4, local copies, waits for them, and re-layouts: 3.14 us -> 1.84 us
where the time goes in v2:
time: 47.6 us; the launch traced here: 47.4 us
  Pallas kernels  45 us (95%)
  local copies, waits for them, and re-layouts  1.84 us (4%)
  between operations  0.65 us (1%)
    pallas_call x1, Pallas kernels, local(): pl.pallas_call(functools.partial(kernel, n_row, n_col), out_shape=(jax.Sh...  45 us
    unnamed x4, local copies, waits for them, and re-layouts  1.84 us

profile of v2, /device:TPU:25, one launch (start us, length us, event | category | flops | bytes accessed | tf_op | source)
XLA Modules:
  0.0 47.4 jit_solution(7652676781646457191)
XLA Ops:
  0.6 45.0 %forward_solve.1 = (f32[1,1,4,1024]{3,2,1,0:T(4,128)}, f32[1,1,4]{2,1,0:T(1,128)}) custom-call(f32[1,1,4,1024]{3,2,1,0:T(4,128)} %rhs_hbm.1, bf16[1,1,256,1024]{3,2,1,0:T(8,128)(2,1)} %inv_hbm.1, bf16[1,1,2,1,128,1024]{5,4,3,2,1,0:T(8,128)(2,1)} %u_hbm.1, bf16[1,1,2,1,128,1024]{5,4,3,2,1,0:T(8,128)(2,1)} %v_hbm.1, s32[2]{0:T(128)} %bitcast.1), custom_call_target="tpu_custom_call" | custom-call | tf_op jit(solution)/shard_map/forward_solve/pallas_call | solution.py:300
  45.6 0.0 copy-start
  45.6 1.3 %copy.9 = f32[1,1,4,1024]{3,2,1,0:T(4,128)} copy(f32[1,1,4,1024]{3,2,1,0:T(4,128)} %get-tuple-element.4) | data formatting | bytes 32768
  46.9 0.0 copy-done
  46.9 0.5 %copy.10 = f32[1,1,4]{2,1,0:T(1,128)} copy(f32[1,1,4]{2,1,0:T(1,128)S(1)} %copy-done) | data formatting | bytes 32
Async XLA Ops:
  45.6 1.3 %copy-start = (f32[1,1,4]{2,1,0:T(1,128)S(1)}, f32[1,1,4]{2,1,0:T(1,128)}, u32[]{:S(2)}) copy-start(f32[1,1,4]{2,1,0:T(1,128)} %get-tuple-element.5) | copy-start | bytes 52

commit v3 on v2

--- a/solution.py
+++ b/solution.py
@@ -10,6 +10,8 @@
 
 MESH = pl.DeviceIdType.MESH
 NT = (((1,), (1,)), ((), ()))
+FIRST_SHORT = 3
+NEAR = 2
 
 
 def remote(src, dst, send_sem, recv_sem, device):
@@ -29,7 +31,7 @@
     white_ref, lik_ref,
     rhs_ref, inv_ref, u_ref, v_ref,
     y_in, p_out, p_in, y_row, logs, base,
-    v_out, v_in, u_out, u_in, fold, w_out, w_in,
+    v_out, v_in, u_out, u_in, fold, w_out, w_in, y_full, y_all,
     in_sem, y_send, y_recv, p_send, p_recv, o_send, o_recv, l_send, l_recv,
     v_send, v_recv, u_send, u_recv, w_send, w_recv,
 ):
@@ -52,10 +54,12 @@
     for copy in copies:
         copy.start()
 
-    short = row >= 2
-    feeds = (row >= 1) & (row < last)
+    short = row >= FIRST_SHORT
+    feeds = (row + 1 >= FIRST_SHORT) & (row < last)
     long_count = jnp.where(short, row - 1, row)
-    long_first = jnp.where(row == 0, 1, row + 2)
+    long_first = jnp.where(feeds, row + 2, row + 1)
+    near_end = jnp.minimum(row + NEAR + 1, n_row)
+    relays = col == own_home
 
     barrier = pltpu.get_barrier_semaphore()
 
@@ -80,20 +84,35 @@
 
     greeted = greeted + jnp.where(row > 0, n_col, 0)
 
-    def greet_later(i, count):
-        greet(i, own_home)
+    for d in range(2, NEAR + 1):
+
+        @pl.when(row + d < n_row)
+        def _():
+            greet(row + d, own_home)
+
+        greeted = greeted + jnp.where(row + d < n_row, 1, 0)
+        fed = (row >= d) & (lax.rem(jnp.maximum(row - d, 0), n_col) == col)
+
+        @pl.when(fed)
+        def _():
+            for s in range(n_col):
+                greet(row - d, s)
+
+        greeted = greeted + jnp.where(fed, n_col, 0)
+
+    def greet_far(i, count):
+        greet(i, col)
         return count + 1
 
-    greeted = lax.fori_loop(row + 2, n_row, greet_later, greeted)
+    greeted = lax.fori_loop(jnp.where(relays, near_end, n_row), n_row, greet_far, greeted)
     for q in range(per_col):
         j = q * n_col + col
 
-        @pl.when(j < row - 1)
-        def _():
-            for s in range(n_col):
-                greet(j, s)
-
-        greeted = greeted + jnp.where(j < row - 1, n_col, 0)
+        @pl.when(j < row - NEAR)
+        def _():
+            greet(j, col)
+
+        greeted = greeted + jnp.where(j < row - NEAR, 1, 0)
 
     prev_slot = jnp.maximum(row - 1, 0) // n_col
     prev_home = lax.rem(jnp.maximum(row - 1, 0), n_col)
@@ -158,11 +177,23 @@
 
         @pl.when(j < long_count)
         def _():
-            for s in range(n_col):
-                remote(y_in.at[q, s], y_in.at[q, s], y_send.at[0], y_recv.at[q, s], (j, s)).wait_recv()
-            y = y_in[q, 0]
-            for s in range(1, n_col):
-                y = y + y_in[q, s]
+            near = row - j <= NEAR
+            remote(y_in.at[q, 0], y_in.at[q, 0], y_send.at[0], y_recv.at[q, 0], (j, col)).wait_recv()
+
+            @pl.when(near)
+            def _():
+                for s in range(1, n_col):
+                    remote(y_in.at[q, s], y_in.at[q, s], y_send.at[0], y_recv.at[q, s], (j, s)).wait_recv()
+                y = y_in[q, 0]
+                for s in range(1, n_col):
+                    y = y + y_in[q, s]
+                y_full[...] = y
+
+            @pl.when(jnp.logical_not(near))
+            def _():
+                y_full[...] = y_in[q, 0]
+
+            y = y_full[...]
             inner = lax.dot_general(y.astype(jnp.bfloat16), v_ref[q], NT, preferred_element_type=jnp.float32)
             keep = lax.broadcasted_iota(jnp.int32, (nrhs, rank_max), 1) < rank_ref[q]
             inner = jnp.where(keep, inner, 0.0).astype(jnp.bfloat16)
@@ -233,7 +264,7 @@
         remote(y_row.at[col], y_in.at[own_slot, col], y_send.at[i], y_recv.at[own_slot, col], (i, own_home)).start()
         return carry
 
-    lax.fori_loop(long_first, n_row, send_y, 0)
+    lax.fori_loop(long_first, near_end, send_y, 0)
     for k, peer in enumerate(peers):
         remote(y_row.at[col], y_row.at[col], o_send.at[k], o_recv.at[col], (row, peer)).start()
     pl.when(row == 0)(log_part)
@@ -245,6 +276,16 @@
     for s in range(1, n_col):
         y = y + y_row[s]
         log_sum = log_sum + logs[s]
+    y_all[...] = y
+
+    def far_copy(i):
+        return remote(y_all, y_in.at[own_slot, 0], y_send.at[i], y_recv.at[own_slot, 0], (i, col))
+
+    def send_far(i, carry):
+        far_copy(i).start()
+        return carry
+
+    lax.fori_loop(jnp.where(relays, near_end, n_row), n_row, send_far, 0)
     white_ref[0, 0] = y
     quadratic = jnp.sum(y * y, axis=1, keepdims=True) * (1.0 / width)
     lik = -0.5 * quadratic + log_sum * (1.0 / width) - 0.5 * math.log(2.0 * math.pi)
@@ -257,7 +298,13 @@
         remote(y_row.at[col], y_in.at[own_slot, col], y_send.at[i], y_recv.at[own_slot, col], (i, own_home)).wait_send()
         return carry
 
-    lax.fori_loop(long_first, n_row, left_y, 0)
+    lax.fori_loop(long_first, near_end, left_y, 0)
+
+    def left_far(i, carry):
+        far_copy(i).wait_send()
+        return carry
+
+    lax.fori_loop(jnp.where(relays, near_end, n_row), n_row, left_far, 0)
     for k, peer in enumerate(peers):
         remote(logs.at[col], logs.at[col], l_send.at[k], l_recv.at[col], (row, peer)).wait_send()
         remote(y_row.at[col], y_row.at[col], o_send.at[k], o_recv.at[col], (row, peer)).wait_send()
@@ -300,8 +347,8 @@
     return pl.pallas_call(
         functools.partial(kernel, n_row, n_col),
         out_shape=(
-            jax.ShapeDtypeStruct((1, 1, nrhs, width), jnp.float32),
-            jax.ShapeDtypeStruct((1, 1, nrhs), jnp.float32),
+            pltpu.VMEM((1, 1, nrhs, width), jnp.float32),
+            pltpu.VMEM((1, 1, nrhs), jnp.float32),
         ),
         in_specs=[hbm, hbm, hbm, hbm, pl.BlockSpec(memory_space=pltpu.SMEM)],
         out_specs=(vmem, vmem),
@@ -323,6 +370,8 @@
             f32(piece, rank_max),
             f32(nrhs, rank_max),
             f32(n_col, nrhs, rank_max),
+            f32(nrhs, width),
+            f32(nrhs, width),
             dma((4,)),
             dma((n_row,)),
             dma((per_col, n_col)),

time: 47.6 us -> 39.1 us (0.82)
  Pallas kernels: 45 us -> 37 us
  local copies, waits for them, and re-layouts: 1.84 us -> 1.12 us
    pallas_call x1, Pallas kernels: 45 us -> 37 us  [local(): pl.pallas_call(functools.partial(kernel, n_row, n_col), out_shape=(pltpu....]
    unnamed x4 -> x2, local copies, waits for them, and re-layouts: 1.84 us -> 1.12 us
where the time goes in v3:
time: 39.1 us; the launch traced here: 38.8 us
  Pallas kernels  37 us (95%)
  local copies, waits for them, and re-layouts  1.12 us (3%)
  between operations  0.64 us (2%)
    pallas_call x1, Pallas kernels, local(): pl.pallas_call(functools.partial(kernel, n_row, n_col), out_shape=(pltpu....  37 us
    unnamed x2, local copies, waits for them, and re-layouts  1.12 us

profile of v3, /device:TPU:25, one launch (start us, length us, event | category | flops | bytes accessed | tf_op | source)
XLA Modules:
  0.0 38.8 jit_solution(12508183896837441970)
XLA Ops:
  0.6 37.0 %forward_solve.1 = (f32[1,1,4,1024]{3,2,1,0:T(4,128)S(1)}, f32[1,1,4]{2,1,0:T(1,128)S(1)}) custom-call(f32[1,1,4,1024]{3,2,1,0:T(4,128)} %rhs_hbm.1, bf16[1,1,256,1024]{3,2,1,0:T(8,128)(2,1)} %inv_hbm.1, bf16[1,1,2,1,128,1024]{5,4,3,2,1,0:T(8,128)(2,1)} %u_hbm.1, bf16[1,1,2,1,128,1024]{5,4,3,2,1,0:T(8,128)(2,1)} %v_hbm.1, s32[2]{0:T(128)} %bitcast.1), custom_call_target="tpu_custom_call" | custom-call | tf_op jit(solution)/shard_map/forward_solve/pallas_call | solution.py:347
  37.7 0.6 %copy.9 = f32[1,1,4,1024]{3,2,1,0:T(4,128)} copy(f32[1,1,4,1024]{3,2,1,0:T(4,128)S(1)} %get-tuple-element.2) | data formatting | bytes 32768
  38.3 0.5 %copy.10 = f32[1,1,4]{2,1,0:T(1,128)} copy(f32[1,1,4]{2,1,0:T(1,128)S(1)} %get-tuple-element.3) | data formatting | bytes 32

commit v4 on v3

--- a/solution.py
+++ b/solution.py
@@ -10,7 +10,7 @@
 
 MESH = pl.DeviceIdType.MESH
 NT = (((1,), (1,)), ((), ()))
-FIRST_SHORT = 3
+FIRST_SHORT = 4
 NEAR = 2
 
 
@@ -33,7 +33,7 @@
     y_in, p_out, p_in, y_row, logs, base,
     v_out, v_in, u_out, u_in, fold, w_out, w_in, y_full, y_all,
     in_sem, y_send, y_recv, p_send, p_recv, o_send, o_recv, l_send, l_recv,
-    v_send, v_recv, u_send, u_recv, w_send, w_recv,
+    v_send, v_recv, u_send, u_recv, w_send, w_recv, m_send, m_recv, f_send,
 ):
     row = lax.axis_index("row")
     col = lax.axis_index("col")
@@ -138,13 +138,39 @@
     def u_copy(k, peer):
         return remote(u_out.at[peer], u_in, u_send.at[k], u_recv, (row, peer))
 
+    crosses = short & (lax.rem(row, 2) == 0)
+
+    def by_way(s):
+        return crosses & (prev_home != s) & (prev_home + s != n_col - 1)
+
+    def way_copy(cc, s):
+        return remote(v_out.at[cc], v_out.at[cc], m_send.at[s], m_recv.at[cc], (row, s))
+
     @pl.when(gives)
     def _():
         for s in range(n_col):
-            v_copy(s, row - 1).start()
+
+            @pl.when(by_way(s))
+            def _():
+                for cc in range(s, n_col):
+                    way_copy(cc, s).start()
+
+            @pl.when(jnp.logical_not(by_way(s)))
+            def _():
+                v_copy(s, row - 1).start()
+
         for k, peer in enumerate(peers):
             u_copy(k, peer).start()
         u_in[...] = u_out[col]
+
+    @pl.when(by_way(col))
+    def _():
+        def forward(cc, carry):
+            remote(v_out.at[cc], v_out.at[cc], m_send.at[0], m_recv.at[cc], (row, prev_home)).wait_recv()
+            remote(v_out.at[cc], v_in.at[cc], f_send, v_recv, (row - 1, col)).start()
+            return carry
+
+        lax.fori_loop(col, n_col, forward, 0)
 
     copies[2].wait()
     copies[3].wait()
@@ -317,9 +343,25 @@
     @pl.when(gives)
     def _():
         for s in range(n_col):
-            v_copy(s, row - 1).wait_send()
+            part = pl.ds(s, n_col - s)
+
+            @pl.when(by_way(s))
+            def _():
+                remote(v_out.at[part], v_out.at[part], m_send.at[s], m_recv.at[0], (row, s)).wait_send()
+
+            @pl.when(jnp.logical_not(by_way(s)))
+            def _():
+                v_copy(s, row - 1).wait_send()
+
         for k, peer in enumerate(peers):
             u_copy(k, peer).wait_send()
+
+    for cc in range(n_col):
+        part = pl.ds(cc, n_col - cc)
+
+        @pl.when(by_way(col) & (col == cc))
+        def _():
+            remote(v_out.at[part], v_in.at[part], f_send, v_recv, (row - 1, cc)).wait_send()
 
     for q in range(per_col):
         j = q * n_col + col
@@ -387,6 +429,9 @@
             dma,
             dma((n_col,)),
             dma((n_col,)),
+            dma((n_col,)),
+            dma((n_col,)),
+            dma,
         ],
         compiler_params=pltpu.CompilerParams(collective_id=0, has_side_effects=True),
         name="forward_solve",

time: 39.1 us -> 37.2 us (0.951)
  Pallas kernels: 37 us -> 35.1 us
    pallas_call x1, Pallas kernels: 37 us -> 35.1 us  [local(): pl.pallas_call(functools.partial(kernel, n_row, n_col), out_shape=(pltpu....]
where the time goes in v4:
time: 37.2 us; the launch traced here: 36.9 us
  Pallas kernels  35.1 us (94%)
  local copies, waits for them, and re-layouts  1.12 us (3%)
  between operations  0.64 us (2%)
    pallas_call x1, Pallas kernels, local(): pl.pallas_call(functools.partial(kernel, n_row, n_col), out_shape=(pltpu....  35.1 us
    unnamed x2, local copies, waits for them, and re-layouts  1.12 us

profile of v4, /device:TPU:25, one launch (start us, length us, event | category | flops | bytes accessed | tf_op | source)
XLA Modules:
  0.0 36.9 jit_solution(16487206383531855768)
XLA Ops:
  0.6 35.1 %forward_solve.1 = (f32[1,1,4,1024]{3,2,1,0:T(4,128)S(1)}, f32[1,1,4]{2,1,0:T(1,128)S(1)}) custom-call(f32[1,1,4,1024]{3,2,1,0:T(4,128)} %rhs_hbm.1, bf16[1,1,256,1024]{3,2,1,0:T(8,128)(2,1)} %inv_hbm.1, bf16[1,1,2,1,128,1024]{5,4,3,2,1,0:T(8,128)(2,1)} %u_hbm.1, bf16[1,1,2,1,128,1024]{5,4,3,2,1,0:T(8,128)(2,1)} %v_hbm.1, s32[2]{0:T(128)} %bitcast.1), custom_call_target="tpu_custom_call" | custom-call | tf_op jit(solution)/shard_map/forward_solve/pallas_call | solution.py:389
  35.7 0.6 %copy.9 = f32[1,1,4,1024]{3,2,1,0:T(4,128)} copy(f32[1,1,4,1024]{3,2,1,0:T(4,128)S(1)} %get-tuple-element.2) | data formatting | bytes 32768
  36.4 0.5 %copy.10 = f32[1,1,4]{2,1,0:T(1,128)} copy(f32[1,1,4]{2,1,0:T(1,128)S(1)} %get-tuple-element.3) | data formatting | bytes 32
